TPU v7x, 32 devices: a whole 2x2x4 slice. The times are simulated.
32 devices in a mesh: cx: 4 (over z), cy: 2 (over y), tp: 4 (over x, core).
Axes of the slice: x: 2, y: 2, z: 4, core: 2. Of those that a mesh axis runs over, the one named last changes fastest.
Arguments:
- neighbor_ids: int32 [16, 8, 128], P(('cx', 'cy'), 'tp'), may hold values from 0 to 1023
- decoder: bfloat16 [16, 64, 896], P(('cx', 'cy')), may hold values from -6 to 6
- table: bfloat16 [1024, 896], P(('cx', 'cy')), may hold values from -6 to 6
- attn_in: bfloat16 [6, 896, 896], P(None, ('cx', 'cy'), 'tp'), may hold values from -0.1875 to 0.1875
- attn_out: bfloat16 [2, 896, 896], P(None, 'tp', ('cx', 'cy')), may hold values from -0.1875 to 0.1875
- gains: float32 [3, 896], replicated, may hold values from 0.25 to 1.75
- w_up: bfloat16 [896, 3584], P(('cx', 'cy'), 'tp'), may hold values from -0.1875 to 0.1875
- w_down: bfloat16 [3584, 896], P('tp', ('cx', 'cy')), may hold values from -0.09375 to 0.09375
Outputs:
- encoded: bfloat16 [16, 8, 128, 896], P(('cx', 'cy'), 'tp')
All inputs are finite; a program needn't handle non-finite values.
Results may differ from a plain program's by a relative error of at most 0.013.
Values may be sent and summed in bfloat16 or wider, within the bound.
No kernel may reach another device: no remote copies, remote signals or barrier semaphores. Data moves between devices by JAX's collectives and lax.ppermute only.
A program may use at most 128 MiB of HBM per device.

v0:
```python
import jax
import jax.numpy as jnp
from jax import lax
from jax.sharding import PartitionSpec as P

HD = 64


def layer_norm(values, gain):
    middle = jnp.mean(values, axis=-1, keepdims=True)
    centred = values - middle
    spread = jnp.mean(centred * centred, axis=-1, keepdims=True)
    return (centred * lax.rsqrt(spread + 1e-05) * gain).astype(jnp.bfloat16)


def project(hidden, matrix):
    return jnp.dot(hidden, matrix, preferred_element_type=jnp.float32).astype(jnp.bfloat16)


def attend(query, key_rows, value_rows):
    batch, q_len, width = query.shape
    k_len = key_rows.shape[1]
    heads = width // HD
    q_heads = query.reshape(batch, q_len, heads, HD)
    k_heads = key_rows.reshape(batch, k_len, heads, HD)
    v_heads = value_rows.reshape(batch, k_len, heads, HD)
    scores = jnp.einsum(
        "bqhd,bkhd->bhqk", q_heads, k_heads, preferred_element_type=jnp.float32
    ) * HD ** (-0.5)
    probs = jax.nn.softmax(scores, axis=-1).astype(jnp.bfloat16)
    mixed = jnp.einsum("bhqk,bkhd->bqhd", probs, v_heads, preferred_element_type=jnp.float32)
    return mixed.reshape(batch, q_len, width).astype(jnp.bfloat16)


def body(neighbor_ids, decoder, table, attn_in, attn_out, gains, w_up, w_down):
    full_table, in_w, out_w, up_w, down_w = (
        lax.all_gather(table, ("cx", "cy"), axis=0, tiled=True),
        lax.all_gather(attn_in, ("cx", "cy"), axis=1, tiled=True),
        lax.all_gather(attn_out, ("cx", "cy"), axis=2, tiled=True),
        lax.all_gather(w_up, ("cx", "cy"), axis=0, tiled=True),
        lax.all_gather(w_down, ("cx", "cy"), axis=1, tiled=True),
    )
    spans, nbrs, length = neighbor_ids.shape
    width = full_table.shape[1]
    dec_len = decoder.shape[1]
    total = spans * nbrs * length
    dec_rows = decoder.reshape(spans * dec_len, width)
    x_zero = jnp.take(full_table, neighbor_ids.reshape(-1), axis=0).astype(jnp.float32)
    h_one = layer_norm(x_zero, gains[0])
    in_full, out_full = (
        lax.all_gather(in_w, "tp", axis=2, tiled=True),
        lax.all_gather(out_w, "tp", axis=1, tiled=True),
    )
    query = project(h_one, in_full[0]).reshape(spans * nbrs, length, width)
    keys = project(h_one, in_full[1]).reshape(spans * nbrs, length, width)
    values = project(h_one, in_full[2]).reshape(spans * nbrs, length, width)
    self_out = attend(query, keys, values).reshape(total, width)
    x_one = x_zero + jnp.dot(self_out, out_full[0], preferred_element_type=jnp.float32)
    h_two = layer_norm(x_one, gains[1])
    cross_q = project(h_two, in_full[3]).reshape(spans, nbrs * length, width)
    cross_k = project(dec_rows, in_full[4]).reshape(spans, dec_len, width)
    cross_v = project(dec_rows, in_full[5]).reshape(spans, dec_len, width)
    cross = attend(cross_q, cross_k, cross_v).reshape(total, width)
    x_two = x_one + jnp.dot(cross, out_full[1], preferred_element_type=jnp.float32)
    h_three = layer_norm(x_two, gains[2])
    every = lax.all_gather(h_three, "tp", axis=0, tiled=True)
    upward = jnp.dot(every, up_w, preferred_element_type=jnp.float32)
    act = jax.nn.gelu(upward, approximate=True).astype(jnp.bfloat16)
    mixed = lax.psum_scatter(
        jnp.dot(act, down_w, preferred_element_type=jnp.float32).astype(jnp.bfloat16),
        "tp",
        scatter_dimension=0,
        tiled=True,
    ).astype(jnp.float32)
    return (x_two + mixed).astype(jnp.bfloat16).reshape(spans, nbrs, length, width)


def solution(mesh):
    in_specs = (
        P(("cx", "cy"), "tp", None),
        P(("cx", "cy"), None, None),
        P(("cx", "cy"), None),
        P(None, ("cx", "cy"), "tp"),
        P(None, "tp", ("cx", "cy")),
        P(),
        P(("cx", "cy"), "tp"),
        P("tp", ("cx", "cy")),
    )
    out_specs = P(("cx", "cy"), "tp", None, None)
    return jax.shard_map(body, mesh=mesh, in_specs=in_specs, out_specs=out_specs, check_vma=False)
```

profile of v0, /device:TPU:0, one launch (start us, length us, event | category | flops | bytes accessed | tf_op | source)
XLA Modules:
  0.0 414.2 jit_solution(9565664598188071752)
XLA Ops:
  9.3 69.2 %all-gather.10.cloned.1.call-done = bf16[6,896,224]{2,0,1:T(8,128)(2,1)} async-done(((bf16[6,112,224]{2,0,1:T(8,128)(2,1)}), bf16[6,896,224]{2,0,1:T(8,128)(2,1)}) %all-gather.10.cloned.1.call-update) | async-done | bytes 2408464 | tf_op jit(solution)/shard_map/all_gather | solution.py:38
  78.5 6.1 %copy.67 = bf16[6,896,224]{1,2,0:T(8,128)(2,1)} copy(bf16[6,896,224]{2,0,1:T(8,128)(2,1)} %all-gather.10.cloned.1.call-done) | data formatting | bytes 4816896 | tf_op jit(solution)/shard_map/all_gather | solution.py:38
  85.6 34.5 %all_gather.27 = bf16[2,224,896]{1,0,2:T(2,128)(2,1)S(1)} all-gather(bf16[2,224,112]{1,0,2:T(2,128)(2,1)S(1)} %copy.76), channel_id=1, replica_groups=mesh['cx'=4,'cy'=2,'tp'=4] {'cx','cy'}, dimensions={2}, use_global_device_ids=true | all-gather | bytes 903168 | tf_op jit(solution)/shard_map/all_gather | solution.py:39
  123.7 7.4 %all-gather.8.cloned.1.call-done = bf16[1024,896]{1,0:T(8,128)(2,1)} async-done(((bf16[128,896]{1,0:T(8,128)(2,1)}), bf16[1024,896]{1,0:T(8,128)(2,1)}) %all-gather.8.cloned.1.call-update) | async-done | bytes 1835024 | tf_op jit(solution)/shard_map/all_gather | solution.py:37
  131.1 4.3 %gather_fusion = bf16[512,896]{1,0:T(8,128)(2,1)S(1)} fusion(bf16[1024,896]{1,0:T(8,128)(2,1)} %all-gather.8.cloned.1.call-done, s32[1024]{0:T(1024)S(1)} %pad_clamp_fusion), kind=kCustom, calls=%fused_computation | custom fusion | bytes 1837056 | tf_op jit(solution)/shard_map/jit(_take)/gather | solution.py:48
  136.2 61.5 %all-gather.12.cloned.1.call-done = bf16[6,896,896]{1,2,0:T(8,128)(2,1)} async-done(((bf16[6,896,224]{1,2,0:T(8,128)(2,1)}), bf16[6,896,896]{1,2,0:T(8,128)(2,1)}) %all-gather.12.cloned.1.call-update) | async-done | bytes 9633808 | tf_op jit(solution)/shard_map/all_gather | solution.py:51
  197.7 3.8 fusion.46
  201.5 2.9 reshape.106
  204.4 3.9 fusion.47
  208.3 4.0 reshape.107
  212.3 3.0 fusion.29
  215.3 2.7 fusion.82
  218.0 3.8 fusion.45
  221.7 3.1 reshape.105
  224.8 2.8 fusion.52
  228.4 2.8 fusion.83
  232.4 2.8 fusion.48
  239.0 2.7 fusion.56
  249.3 2.8 fusion.85
  253.7 21.0 %all-gather.18.cloned.1.call-done = bf16[896,896]{1,0:T(8,128)(2,1)} async-done(((bf16[112,896]{1,0:T(8,128)(2,1)}), bf16[896,896]{1,0:T(8,128)(2,1)}) %all-gather.18.cloned.1.call-update) | async-done | bytes 1605648 | tf_op jit(solution)/shard_map/all_gather | solution.py:40
  274.7 45.0 %all-gather.20.cloned.1.call-done = bf16[896,896]{0,1:T(8,128)(2,1)} async-done(((bf16[896,112]{0,1:T(8,128)(2,1)}), bf16[896,896]{0,1:T(8,128)(2,1)}) %all-gather.20.cloned.1.call-update) | async-done | bytes 1605648 | tf_op jit(solution)/shard_map/all_gather | solution.py:41
  319.7 31.4 %all-gather.16.cloned.1.call-done = bf16[2048,896]{1,0:T(8,128)(2,1)} async-done(((bf16[512,896]{1,0:T(8,128)(2,1)}), bf16[2048,896]{1,0:T(8,128)(2,1)}) %all-gather.16.cloned.1.call-update) | async-done | bytes 3670032 | tf_op jit(solution)/shard_map/all_gather | solution.py:66
  351.1 12.6 %fusion.16 = bf16[2048,896]{1,0:T(8,128)(2,1)} fusion(bf16[896,896]{0,1:T(8,128)(2,1)} %all-gather.20.cloned.1.call-done, bf16[2048,896]{1,0:T(8,128)(2,1)} %all-gather.16.cloned.1.call-done, bf16[896,896]{1,0:T(8,128)(2,1)} %all-gather.18.cloned.1.call-done), kind=kOutput, calls=%fused_computation.19 | convolution fusion | flops 6595018752 | bytes 10551296 | tf_op jit(solution)/shard_map/dot_general | solution.py:70
  363.7 41.4 %reduce-scatter.2.cloned.1.call-done = bf16[512,896]{1,0:T(8,128)(2,1)} async-done(((bf16[2048,896]{1,0:T(8,128)(2,1)}), bf16[512,896]{1,0:T(8,128)(2,1)}) %reduce-scatter.2.cloned.1.call-update) | async-done | bytes 917520 | tf_op jit(solution)/shard_map/reduce_scatter | solution.py:69
  (62 shorter events, 25.3 us)
Async XLA Ops:
  6.5 230.0 %copy-start = (bf16[2,64,896]{2,1,0:T(8,128)(2,1)S(1)}, bf16[2,64,896]{2,1,0:T(8,128)(2,1)}, u32[]{:S(2)}) copy-start(bf16[2,64,896]{2,1,0:T(8,128)(2,1)} %param.9) | copy-start | bytes 688132
  6.5 71.9 %all-gather.10.cloned.1.call-start = ((), (), s32[]{:S(2)}) async-start(), calls=%async_computation.2 | async-start | bytes 4128768 | tf_op jit(solution)/shard_map/all_gather | solution.py:38
  8.5 122.6 %all-gather.8.cloned.1.call-start = ((), (), s32[]{:S(2)}) async-start(), calls=%async_computation.1 | async-start | bytes 2064384 | tf_op jit(solution)/shard_map/all_gather | solution.py:37
  9.2 188.5 %all-gather.12.cloned.1.call-start = ((), (), s32[]{:S(2)}) async-start(), calls=%async_computation.3 | async-start | bytes 12042240 | tf_op jit(solution)/shard_map/all_gather | solution.py:51
  84.6 0.9 copy-start.5
  84.6 143.8 %all-gather.14.cloned.1.call-start = ((), (), s32[]{:S(2)}) async-start(), calls=%async_computation.4 | async-start | bytes 4014080 | tf_op jit(solution)/shard_map/all_gather | solution.py:52
  85.6 38.0 %copy-start.6 = (s32[2,2,128]{2,1,0:T(2,128)S(1)}, s32[2,2,128]{2,1,0:T(2,128)}, u32[]{:S(2)}) copy-start(s32[2,2,128]{2,1,0:T(2,128)} %param.8) | copy-start | bytes 6148
  85.6 38.0 %copy-start.7 = (f32[3,896]{1,0:T(4,128)S(1)}, f32[3,896]{1,0:T(4,128)}, u32[]{:S(2)}) copy-start(f32[3,896]{1,0:T(4,128)} %param.13) | copy-start | bytes 32260
  122.4 152.3 %all-gather.18.cloned.1.call-start = ((), (), s32[]{:S(2)}) async-start(), calls=%async_computation.6 | async-start | bytes 1806336 | tf_op jit(solution)/shard_map/all_gather | solution.py:40
  122.9 196.7 %all-gather.20.cloned.1.call-start = ((), (), s32[]{:S(2)}) async-start(), calls=%async_computation.7 | async-start | bytes 1806336 | tf_op jit(solution)/shard_map/all_gather | solution.py:41
  123.5 227.6 %all-gather.16.cloned.1.call-start = ((), (), s32[]{:S(2)}) async-start(), calls=%async_computation.5 | async-start | bytes 4587520 | tf_op jit(solution)/shard_map/all_gather | solution.py:66
  231.2 1.2 copy-start.2
  243.8 1.3 copy-start.4
  247.8 1.5 copy-start.3
  253.7 151.4 %reduce-scatter.2.cloned.1.call-start = ((), (), s32[]{:S(2)}) async-start(), calls=%async_computation.8 | async-start | bytes 4587520 | tf_op jit(solution)/shard_map/reduce_scatter | solution.py:69
  363.7 43.6 %copy-start.1 = (bf16[2,64,896]{2,1,0:T(8,128)(2,1)S(1)}, bf16[2,64,896]{2,1,0:T(8,128)(2,1)}, u32[]{:S(2)}) copy-start(bf16[2,64,896]{2,1,0:T(8,128)(2,1)} %param.9) | copy-start | bytes 688132
Sparse Core Ops, SparseCore 0:
  9.5 68.9 all-gather.9
  80.7 50.3 all-gather.7
  132.6 65.0 all-gather.11
  199.1 28.8 all-gather.13
  230.1 44.5 all-gather.17
  276.7 42.9 all-gather.19
  321.2 29.8 all-gather.15
  363.8 41.2 reduce-scatter.1
where the time goes:
time: 415 us; the launch traced here: 414 us
  waiting for transfers between devices  279 us (67%)
  matrix products  45.8 us (11%)
  blocking collectives  34.5 us (8%)
  local copies, waits for them, and re-layouts  32.9 us (8%)
  between operations  13.7 us (3%)
  other arithmetic  8.18 us (2%)
    all_gather x1, waiting for transfers between devices, body(): lax.all_gather(attn_in, ('cx', 'cy'), axis=1, tiled=True)  69.2 us
    all_gather x1, waiting for transfers between devices, body(): lax.all_gather(in_w, 'tp', axis=2, tiled=True)  61.5 us
    all_gather x1, waiting for transfers between devices, body(): lax.all_gather(w_down, ('cx', 'cy'), axis=1, tiled=True)  45 us
    reduce_scatter x1, waiting for transfers between devices, body(): lax.psum_scatter(jnp.dot(act, down_w, preferred_element_type=jnp.float32)...  41.4 us
    all_gather x1, blocking collectives, body(): lax.all_gather(attn_out, ('cx', 'cy'), axis=2, tiled=True)  34.5 us
    all_gather x1, waiting for transfers between devices, body(): every = lax.all_gather(h_three, 'tp', axis=0, tiled=True)  31.4 us
    all_gather x1, waiting for transfers between devices, body(): lax.all_gather(w_up, ('cx', 'cy'), axis=0, tiled=True)  21 us
    dot_general x6, matrix products, project(): jnp.dot(hidden, matrix, preferred_element_type=jnp.float32)  18.9 us
  transfers between devices with their start and end apart: 8, of which 7 were waited for; matrix products, arithmetic and copies ran while one was open for 16% of the time, Pallas kernels for 0%

commit v1 on v0

--- a/solution.py
+++ b/solution.py
@@ -63,7 +63,21 @@
     cross = attend(cross_q, cross_k, cross_v).reshape(total, width)
     x_two = x_one + jnp.dot(cross, out_full[1], preferred_element_type=jnp.float32)
     h_three = layer_norm(x_two, gains[2])
-    every = lax.all_gather(h_three, "tp", axis=0, tiled=True)
+
+    def _launch_knots(mat, ndim_at=0):
+        degree = lax.axis_size("tp")
+        arrivals = [mat]
+        for i in range(degree - 1):
+            current_arr = lax.ppermute(
+                arrivals[-1], "tp", [(d, (d + 1) % degree) for d in range(degree)]
+            )
+            arrivals.append(current_arr)
+        z2 = jnp.concatenate(arrivals[::-1], axis=ndim_at)
+        small = lax.axis_index("tp")
+        ready = jnp.roll(z2, shift=(small + 1) * mat.shape[ndim_at], axis=ndim_at)
+        return ready
+
+    every = _launch_knots(h_three)
     upward = jnp.dot(every, up_w, preferred_element_type=jnp.float32)
     act = jax.nn.gelu(upward, approximate=True).astype(jnp.bfloat16)
     mixed = lax.psum_scatter(

time: 415 us -> 383 us (0.923)
  waiting for transfers between devices: 279 us -> 235 us
  local copies, waits for them, and re-layouts: 32.9 us -> 43 us
    ppermute x0 -> x3, waiting for transfers between devices: none -> 38.6 us  [_launch_knots(): lax.ppermute(arrivals[-1], 'tp', [(d, (d + 1) % degree) for d in range(de...]
    all_gather x1 -> x0, waiting for transfers between devices: 31.4 us -> none  [body(): every = lax.all_gather(h_three, 'tp', axis=0, tiled=True)]
    all_gather x1, waiting for transfers between devices: 45 us -> 16.1 us  [body(): lax.all_gather(w_down, ('cx', 'cy'), axis=1, tiled=True)]
    all_gather x1, waiting for transfers between devices: 21 us -> 0.01 us  [body(): lax.all_gather(w_up, ('cx', 'cy'), axis=0, tiled=True)]
    unnamed x19 -> x25, local copies, waits for them, and re-layouts: 5.52 us -> 16.5 us
  transfers between devices with their start and end apart: 8 -> 10, of which waited for: 7 -> 8; matrix products, arithmetic and copies ran while one was open for 16% -> 20% of each run, Pallas kernels for 0% -> 0%
where the time goes in v1:
time: 383 us; the launch traced here: 382 us
  waiting for transfers between devices  235 us (61%)
  matrix products  45.1 us (12%)
  local copies, waits for them, and re-layouts  43 us (11%)
  blocking collectives  34.4 us (9%)
  between operations  13.8 us (4%)
  other arithmetic  9.73 us (3%)
    all_gather x1, waiting for transfers between devices, body(): lax.all_gather(attn_in, ('cx', 'cy'), axis=1, tiled=True)  69.2 us
    all_gather x1, waiting for transfers between devices, body(): lax.all_gather(in_w, 'tp', axis=2, tiled=True)  62 us
    reduce_scatter x1, waiting for transfers between devices, body(): lax.psum_scatter(jnp.dot(act, down_w, preferred_element_type=jnp.float32)...  39.7 us
    ppermute x3, waiting for transfers between devices, _launch_knots(): lax.ppermute(arrivals[-1], 'tp', [(d, (d + 1) % degree) for d in range(de...  38.6 us
    all_gather x1, blocking collectives, body(): lax.all_gather(attn_out, ('cx', 'cy'), axis=2, tiled=True)  34.4 us
    dot_general x6, matrix products, project(): jnp.dot(hidden, matrix, preferred_element_type=jnp.float32)  18.2 us
    unnamed x25, local copies, waits for them, and re-layouts  16.5 us
    all_gather x1, waiting for transfers between devices, body(): lax.all_gather(w_down, ('cx', 'cy'), axis=1, tiled=True)  16.1 us
  transfers between devices with their start and end apart: 10, of which 8 were waited for; matrix products, arithmetic and copies ran while one was open for 20% of the time, Pallas kernels for 0%

profile of v1, /device:TPU:0, one launch (start us, length us, event | category | flops | bytes accessed | tf_op | source)
XLA Modules:
  0.0 381.5 jit_solution(16135998232159568422)
XLA Ops:
  9.3 69.2 %all-gather.9.cloned.1.call-done = bf16[6,896,224]{2,0,1:T(8,128)(2,1)} async-done(((bf16[6,112,224]{2,0,1:T(8,128)(2,1)}), bf16[6,896,224]{2,0,1:T(8,128)(2,1)}) %all-gather.9.cloned.1.call-update) | async-done | bytes 2408464 | tf_op jit(solution)/shard_map/all_gather | solution.py:38
  78.5 6.1 %copy.67 = bf16[6,896,224]{1,2,0:T(8,128)(2,1)} copy(bf16[6,896,224]{2,0,1:T(8,128)(2,1)} %all-gather.9.cloned.1.call-done) | data formatting | bytes 4816896 | tf_op jit(solution)/shard_map/all_gather | solution.py:38
  85.7 34.4 %all_gather.24 = bf16[2,224,896]{1,0,2:T(2,128)(2,1)S(1)} all-gather(bf16[2,224,112]{1,0,2:T(2,128)(2,1)S(1)} %copy.76), channel_id=1, replica_groups=mesh['cx'=4,'cy'=2,'tp'=4] {'cx','cy'}, dimensions={2}, use_global_device_ids=true | all-gather | bytes 903168 | tf_op jit(solution)/shard_map/all_gather | solution.py:39
  123.1 8.0 %all-gather.7.cloned.1.call-done = bf16[1024,896]{1,0:T(8,128)(2,1)} async-done(((bf16[128,896]{1,0:T(8,128)(2,1)}), bf16[1024,896]{1,0:T(8,128)(2,1)}) %all-gather.7.cloned.1.call-update) | async-done | bytes 1835024 | tf_op jit(solution)/shard_map/all_gather | solution.py:37
  131.1 4.3 %gather_fusion = bf16[512,896]{1,0:T(8,128)(2,1)S(1)} fusion(bf16[1024,896]{1,0:T(8,128)(2,1)} %all-gather.7.cloned.1.call-done, s32[1024]{0:T(1024)S(1)} %pad_clamp_fusion), kind=kCustom, calls=%fused_computation | custom fusion | bytes 1837056 | tf_op jit(solution)/shard_map/jit(_take)/gather | solution.py:48
  136.2 62.0 %all-gather.11.cloned.1.call-done = bf16[6,896,896]{1,2,0:T(8,128)(2,1)} async-done(((bf16[6,896,224]{1,2,0:T(8,128)(2,1)}), bf16[6,896,896]{1,2,0:T(8,128)(2,1)}) %all-gather.11.cloned.1.call-update) | async-done | bytes 9633808 | tf_op jit(solution)/shard_map/all_gather | solution.py:51
  198.2 3.8 fusion.52
  202.0 2.9 reshape.106
  204.9 3.9 %fusion.53 = bf16[512,896]{1,0:T(8,128)(2,1)} fusion(bf16[6,896,896]{1,2,0:T(8,128)(2,1)} %all-gather.11.cloned.1.call-done, f32[896]{0:T(1024)S(1)} %get-tuple-element.6, f32[512]{0:T(512)S(1)} %add_rsqrt_fusion.2, f32[512]{0:T(512)S(1)} %broadcast_multiply_fusion.2, bf16[512,896]{1,0:T(8,128)(2,1)S(1)} %gather_fusion, pred[512]{0:T(512)(128)(4,1)S(1)} %compare_and_fusion), kind=kOutput, calls=%fused_computation.68 | convolution fusion | flops 825294848 | bytes 3448832 | tf_op jit(solution)/shard_map/dot_general | solution.py:17
  208.8 4.0 %reshape.107 = bf16[4,128,14,64]{3,2,1,0:T(8,128)(2,1)} reshape(bf16[512,896]{1,0:T(8,128)(2,1)} %fusion.53) | data formatting | bytes 1835008 | tf_op jit(solution)/shard_map/reshape;reshape | solution.py:25
  212.8 3.0 fusion.31
  215.8 2.7 fusion.90
  218.5 3.8 fusion.51
  222.2 3.1 reshape.105
  225.3 2.8 fusion.58
  228.9 2.8 fusion.91
  232.9 2.8 fusion.54
  248.2 2.8 fusion.93
  251.9 12.6 %collective-permute-done = bf16[512,896]{1,0:T(8,128)(2,1)S(1)} collective-permute-done((bf16[512,896]{1,0:T(8,128)(2,1)S(1)}, bf16[512,896]{1,0:T(8,128)(2,1)S(1)}, u32[]{:S(2)}, u32[]{:S(2)}) %collective-permute-start) | collective-permute-done | bytes 917536 | tf_op jit(solution)/shard_map/ppermute | solution.py:71
  264.6 12.8 %collective-permute-done.1 = bf16[512,896]{1,0:T(8,128)(2,1)} collective-permute-done((bf16[512,896]{1,0:T(8,128)(2,1)S(1)}, bf16[512,896]{1,0:T(8,128)(2,1)}, u32[]{:S(2)}, u32[]{:S(2)}) %collective-permute-start.1) | collective-permute-done | bytes 917536 | tf_op jit(solution)/shard_map/ppermute | solution.py:71
  277.5 13.1 %collective-permute-done.2 = bf16[512,896]{1,0:T(8,128)(2,1)} collective-permute-done((bf16[512,896]{1,0:T(8,128)(2,1)}, bf16[512,896]{1,0:T(8,128)(2,1)}, u32[]{:S(2)}, u32[]{:S(2)}) %collective-permute-start.2) | collective-permute-done | bytes 917536 | tf_op jit(solution)/shard_map/ppermute | solution.py:71
  303.9 16.1 %all-gather.17.cloned.1.call-done = bf16[896,896]{0,1:T(8,128)(2,1)} async-done(((bf16[896,112]{0,1:T(8,128)(2,1)}), bf16[896,896]{0,1:T(8,128)(2,1)}) %all-gather.17.cloned.1.call-update) | async-done | bytes 1605648 | tf_op jit(solution)/shard_map/all_gather | solution.py:41
  320.1 12.6 %fusion.18 = bf16[2048,896]{1,0:T(8,128)(2,1)} fusion(bf16[896,896]{0,1:T(8,128)(2,1)} %all-gather.17.cloned.1.call-done, bf16[896,896]{1,0:T(8,128)(2,1)} %all-gather.15.cloned.1.call-done, bf16[4096,896]{1,0:T(8,128)(2,1)} %constant_dynamic-update-slice_fusion, s32[]{:T(128)S(6)} %select_n.37), kind=kOutput, calls=%fused_computation.21 | convolution fusion | flops 6595018752 | bytes 10551300 | tf_op jit(solution)/shard_map/dot_general | solution.py:84
  332.7 39.7 %reduce-scatter.2.cloned.1.call-done = bf16[512,896]{1,0:T(8,128)(2,1)} async-done(((bf16[2048,896]{1,0:T(8,128)(2,1)}), bf16[512,896]{1,0:T(8,128)(2,1)}) %reduce-scatter.2.cloned.1.call-update) | async-done | bytes 917520 | tf_op jit(solution)/shard_map/reduce_scatter | solution.py:83
  (73 shorter events, 38.5 us)
Async XLA Ops:
  6.5 230.6 %copy-start = (bf16[2,64,896]{2,1,0:T(8,128)(2,1)S(1)}, bf16[2,64,896]{2,1,0:T(8,128)(2,1)}, u32[]{:S(2)}) copy-start(bf16[2,64,896]{2,1,0:T(8,128)(2,1)} %param.9) | copy-start | bytes 688132
  6.5 71.9 %all-gather.9.cloned.1.call-start = ((), (), s32[]{:S(2)}) async-start(), calls=%async_computation.2 | async-start | bytes 4128768 | tf_op jit(solution)/shard_map/all_gather | solution.py:38
  8.5 122.6 %all-gather.7.cloned.1.call-start = ((), (), s32[]{:S(2)}) async-start(), calls=%async_computation.1 | async-start | bytes 2064384 | tf_op jit(solution)/shard_map/all_gather | solution.py:37
  9.2 189.0 %all-gather.11.cloned.1.call-start = ((), (), s32[]{:S(2)}) async-start(), calls=%async_computation.3 | async-start | bytes 12042240 | tf_op jit(solution)/shard_map/all_gather | solution.py:51
  84.6 0.9 copy-start.5
  84.6 144.3 %all-gather.13.cloned.1.call-start = ((), (), s32[]{:S(2)}) async-start(), calls=%async_computation.4 | async-start | bytes 4014080 | tf_op jit(solution)/shard_map/all_gather | solution.py:52
  85.6 37.4 %copy-start.6 = (s32[2,2,128]{2,1,0:T(2,128)S(1)}, s32[2,2,128]{2,1,0:T(2,128)}, u32[]{:S(2)}) copy-start(s32[2,2,128]{2,1,0:T(2,128)} %param.8) | copy-start | bytes 6148
  85.6 37.4 %copy-start.7 = (f32[3,896]{1,0:T(4,128)S(1)}, f32[3,896]{1,0:T(4,128)}, u32[]{:S(2)}) copy-start(f32[3,896]{1,0:T(4,128)} %param.13) | copy-start | bytes 32260
  122.3 181.6 %all-gather.15.cloned.1.call-start = ((), (), s32[]{:S(2)}) async-start(), calls=%async_computation.5 | async-start | bytes 1806336 | tf_op jit(solution)/shard_map/all_gather | solution.py:40
  122.9 197.1 %all-gather.17.cloned.1.call-start = ((), (), s32[]{:S(2)}) async-start(), calls=%async_computation.6 | async-start | bytes 1806336 | tf_op jit(solution)/shard_map/all_gather | solution.py:41
  231.7 1.3 copy-start.2
  240.3 1.2 copy-start.4
  246.7 1.5 copy-start.3
  251.7 12.9 %collective-permute-start = (bf16[512,896]{1,0:T(8,128)(2,1)S(1)}, bf16[512,896]{1,0:T(8,128)(2,1)S(1)}, u32[]{:S(2)}, u32[]{:S(2)}) collective-permute-start(bf16[512,896]{1,0:T(8,128)(2,1)S(1)} %multiply_convert_fusion), channel_id=1, source_target_pairs={{0,1},{1,2},{2,3},{3,0},{4,5},{5,6},{6,7},{7,4},{8,9},{9,10},{10,1... | collective-permute-start | bytes 2752520 | tf_op jit(solution)/shard_map/ppermute | solution.py:71
  264.5 12.9 %collective-permute-start.1 = (bf16[512,896]{1,0:T(8,128)(2,1)S(1)}, bf16[512,896]{1,0:T(8,128)(2,1)}, u32[]{:S(2)}, u32[]{:S(2)}) collective-permute-start(bf16[512,896]{1,0:T(8,128)(2,1)S(1)} %collective-permute-done), channel_id=1, source_target_pairs={{0,1},{1,2},{2,3},{3,0},{4,5},{5,6},{6,7},{7,4},{8,9},{9,10},{10,1... | collective-permute-start | bytes 2752520 | tf_op jit(solution)/shard_map/ppermute | solution.py:71
  264.6 107.9 %reduce-scatter.2.cloned.1.call-start = ((), (), s32[]{:S(2)}) async-start(), calls=%async_computation.7 | async-start | bytes 4587520 | tf_op jit(solution)/shard_map/reduce_scatter | solution.py:83
  277.4 13.1 %collective-permute-start.2 = (bf16[512,896]{1,0:T(8,128)(2,1)}, bf16[512,896]{1,0:T(8,128)(2,1)}, u32[]{:S(2)}, u32[]{:S(2)}) collective-permute-start(bf16[512,896]{1,0:T(8,128)(2,1)} %collective-permute-done.1), channel_id=1, source_target_pairs={{0,1},{1,2},{2,3},{3,0},{4,5},{5,6},{6,7},{7,4},{8,9},{9,10},{10,1... | collective-permute-start | bytes 2752520 | tf_op jit(solution)/shard_map/ppermute | solution.py:71
  332.7 42.0 %copy-start.1 = (bf16[2,64,896]{2,1,0:T(8,128)(2,1)S(1)}, bf16[2,64,896]{2,1,0:T(8,128)(2,1)}, u32[]{:S(2)}) copy-start(bf16[2,64,896]{2,1,0:T(8,128)(2,1)} %param.9) | copy-start | bytes 688132
Sparse Core Ops, SparseCore 0:
  9.5 68.9 all-gather.8
  80.7 50.3 all-gather.6
  132.7 65.5 all-gather.10
  199.6 28.8 all-gather.12
  230.6 44.5 all-gather.14
  277.2 42.8 all-gather.16
  332.8 39.5 reduce-scatter.1
